TPU v7x, 32 devices: a whole 2x2x4 slice. The times are simulated.
32 devices in a mesh: section: 2 (over y), pen: 8 (over z, x), slab: 2 (over core).
Axes of the slice: x: 2, y: 2, z: 4, core: 2. Of those that a mesh axis runs over, the one named last changes fastest.
Arguments:
- velocity: float32 [3, 48, 48, 48], P(None, ('section', 'pen'), 'slab'), may hold values from -6 to 6
- vorticity: float32 [3, 48, 48, 48], P(None, ('section', 'pen'), 'slab'), may hold values from -6 to 6
- velocity_modes: float32 [3, 32, 32, 2, 32], P(None, None, ('section', 'pen'), None, 'slab'), may hold values from -6 to 6
Outputs:
- rhs_modes: float32 [3, 32, 32, 2, 32], P(None, None, ('section', 'pen'), None, 'slab')
All inputs are finite; a program needn't handle non-finite values.
Results may differ from a plain program's by a relative error of at most 0.000057.
Values sent between devices are 32-bit elements; how exact they have to be, the bound alone decides.
A program may use at most 64 MiB of HBM per device.

v0:
```python
import math
import jax
import jax.numpy as jnp
from jax import lax
from jax.sharding import PartitionSpec as P

highest = lax.Precision.HIGHEST


def signed_modes(index, count):
    return jnp.where(index < count // 2, index, index - count)


def discrete_fourier_tables(length, keep_count):
    modes = signed_modes(jnp.arange(keep_count, dtype=jnp.int32), keep_count)
    mode_positions = jnp.arange(length, dtype=jnp.int32)
    phase = jnp.remainder(modes[:, None] * mode_positions[None, :], length).astype(jnp.float32)
    angles = 2.0 * math.pi / length * phase
    factor = 1.0 / math.sqrt(length)
    return (jnp.cos(angles) * factor, jnp.sin(angles) * factor)


def complex_apply(form, cosine, sine, real_part, imag_part):
    out_real = jnp.einsum(form, cosine, real_part, precision=highest) + jnp.einsum(
        form, sine, imag_part, precision=highest
    )
    out_imag = jnp.einsum(form, cosine, imag_part, precision=highest) - jnp.einsum(
        form, sine, real_part, precision=highest
    )
    return (out_real, out_imag)


def per_device(velocity, vorticity, velocity_modes):
    grid_cells = velocity.shape[3]
    keep_count = velocity_modes.shape[1]
    cross_product = jnp.stack(
        [
            velocity[1] * vorticity[2] - velocity[2] * vorticity[1],
            velocity[2] * vorticity[0] - velocity[0] * vorticity[2],
            velocity[0] * vorticity[1] - velocity[1] * vorticity[0],
        ]
    )
    slabs = lax.axis_size("slab")
    block_modes = keep_count // slabs
    cosine_table, sine_table = discrete_fourier_tables(grid_cells, keep_count)
    cols_real = cosine_table.T.reshape(grid_cells, slabs, block_modes)
    cols_imag = (-sine_table).T.reshape(grid_cells, slabs, block_modes)
    column_table = jnp.stack([cols_real, cols_imag], axis=2).reshape(grid_cells, 2 * keep_count)
    first_pass = jnp.einsum("czyx,xj->czyj", cross_product, column_table, precision=highest)
    block = lax.all_to_all(first_pass, "slab", split_axis=3, concat_axis=2, tiled=True)
    out_real, out_imag = complex_apply(
        "ky,czyj->czkj",
        cosine_table,
        sine_table,
        block[..., :block_modes],
        block[..., block_modes:],
    )
    second_pass = jnp.concatenate([out_real, out_imag], axis=-1)
    halves = lax.axis_size("section")
    pens = lax.axis_size("pen")
    rows_ky = keep_count // (halves * pens)
    block = lax.all_to_all(second_pass, ("section", "pen"), split_axis=2, concat_axis=1, tiled=True)
    out_real, out_imag = complex_apply(
        "kz,czyj->ckyj",
        cosine_table,
        sine_table,
        block[..., :block_modes],
        block[..., block_modes:],
    )
    third_pass = jnp.concatenate([out_real, out_imag], axis=-1)
    group_index = lax.axis_index("section") * pens + lax.axis_index("pen")
    modes_z = signed_modes(jnp.arange(keep_count, dtype=jnp.int32), keep_count)[:, None, None]
    modes_y = signed_modes(
        group_index * rows_ky + jnp.arange(rows_ky, dtype=jnp.int32), keep_count
    )[None, :, None]
    modes_x = signed_modes(
        lax.axis_index("slab") * block_modes + jnp.arange(block_modes, dtype=jnp.int32), keep_count
    )[None, None, :]
    limit = -(keep_count // 2)
    keep_mask = ((modes_x != limit) & (modes_y != limit) & (modes_z != limit)).astype(jnp.float32)
    waves = (modes_x.astype(jnp.float32), modes_y.astype(jnp.float32), modes_z.astype(jnp.float32))
    ksq = waves[0] * waves[0] + waves[1] * waves[1] + waves[2] * waves[2]
    denom = jnp.maximum(ksq, 1.0)
    parts = []
    for which in range(2):
        chosen = third_pass[..., which * block_modes : (which + 1) * block_modes]
        comp = [chosen[c] for c in range(3)]
        inner = (waves[0] * comp[0] + waves[1] * comp[1] + waves[2] * comp[2]) / denom
        parts.append(jnp.stack([comp[c] - waves[c] * inner for c in range(3)]))
    projected = jnp.stack(parts, axis=3)
    visc = 0.5 / (keep_count // 2) ** 2
    return (
        projected * keep_mask[None, :, :, None, :]
        - visc * ksq[None, :, :, None, :] * velocity_modes
    )


def solution(mesh):
    return jax.shard_map(
        per_device,
        mesh=mesh,
        in_specs=(
            P(None, ("section", "pen"), "slab", None),
            P(None, ("section", "pen"), "slab", None),
            P(None, None, ("section", "pen"), None, "slab"),
        ),
        out_specs=P(None, None, ("section", "pen"), None, "slab"),
        check_vma=False,
    )
```

profile of v0, /device:TPU:0, one launch (start us, length us, event | category | flops | bytes accessed | tf_op | source)
XLA Modules:
  0.0 32.4 jit_solution(18080253306396795170)
XLA Ops:
  0.0 0.2 cosine_multiply_fusion.1
  0.2 0.9 %multiply_subtract_fusion.2 = (f32[1,3,24,48]{3,2,1,0:T(8,128)S(1)}, f32[1,3,24,48]{3,2,1,0:T(8,128)S(1)}, f32[1,3,24,48]{3,2,1,0:T(8,128)S(1)}) fusion(f32[3,3,24,48]{3,2,1,0:T(8,128)} %param.4, f32[3,3,24,48]{3,2,1,0:T(8,128)} %param.3), kind=kLoop, calls=%fused_computation.28 | loop fusion | flops 31104 | bytes 124416 | tf_op jit(solution)/shard_map/sub | solution.py:38
  1.1 0.3 %fusion.10 = f32[3,3,24,64]{3,2,1,0:T(8,128)S(1)} fusion(f32[48,64,1,1]{0,1,3,2:T(8,128)S(1)} %bitcast.64, f32[1,3,24,48]{3,2,1,0:T(8,128)S(1)} %get-tuple-element.10, f32[1,3,24,48]{3,2,1,0:T(8,128)S(1)} %get-tuple-element.11, f32[1,3,24,48]{3,2,1,0:T(8,128)S(1)} %get-tuple-element.9), kind=kOutput, calls=%fused_computation.15 | convolution fusion | flops 7983360 | bytes 109056 | tf_op jit(solution)/shard_map/czyx,xj->czyj/dot_general | solution.py:49
  1.4 0.2 copy.19
  1.6 0.9 %reshape.210 = f32[2,1,6912]{2,1,0:T(1,128)} reshape(f32[64,3,3,24]{3,2,1,0:T(4,128)S(1)} %bitcast.59) | data formatting | bytes 110592
  2.6 3.3 %all-to-all-start = ((f32[2,1,6912]{2,1,0:T(1,128)}), f32[2,1,6912]{2,1,0:T(1,128)S(1)}, u32[]{:S(2)}, u32[]{:S(2)}) async-start(f32[2,1,6912]{2,1,0:T(1,128)} %reshape.210), calls=%async_computation | async-start | bytes 110592 | tf_op jit(solution)/shard_map/all_to_all | solution.py:50
  5.9 1.4 %all-to-all-done = f32[2,1,6912]{2,1,0:T(1,128)S(1)} async-done(((f32[2,1,6912]{2,1,0:T(1,128)}), f32[2,1,6912]{2,1,0:T(1,128)S(1)}, u32[]{:S(2)}, u32[]{:S(2)}) %all-to-all-start) | async-done | bytes 55328 | tf_op jit(solution)/shard_map/all_to_all | solution.py:50
  7.2 0.5 %broadcast.464 = f32[]{:T(128)} broadcast(f32[]{:T(128)} %constant.195), dimensions={} | broadcast | bytes 8 | tf_op jit(solution)/shard_map/all_to_all | solution.py:50
  7.7 0.7 %reduce = f32[2,6912]{1,0:T(2,128)S(1)} reduce(f32[2,1,6912]{2,1,0:T(1,128)S(1)} %all-to-all-done, f32[]{:T(128)} %broadcast.464), dimensions={1}, to_apply=%all_to_all.26.reduce_sub_computation | reduce | bytes 110596 | tf_op jit(solution)/shard_map/all_to_all | solution.py:50
  8.5 0.3 reshape.211
  8.8 0.2 copy.20
  8.9 0.5 %fusion.7 = f32[3,3,16,32]{3,2,1,0:T(8,128)S(1)} fusion(f32[3,3,48,32]{3,2,1,0:T(8,128)S(1)} %bitcast.54, s32[32]{0:T(128)S(1)} %compare_select_fusion.3), kind=kOutput, calls=%fused_computation.11 | convolution fusion | flops 2669568 | bytes 73856 | tf_op jit(solution)/shard_map/ky,czyj->czkj/dot_general | solution.py:24
  9.5 0.6 %fusion.5 = f32[3,3,16,32]{3,2,1,0:T(8,128)S(1)} fusion(f32[3,3,48,32]{3,2,1,0:T(8,128)S(1)} %bitcast.55, s32[32]{0:T(128)S(1)} %compare_select_fusion.3), kind=kOutput, calls=%fused_computation.9 | convolution fusion | flops 2669568 | bytes 73856 | tf_op jit(solution)/shard_map/ky,czyj->czkj/dot_general | solution.py:27
  10.1 0.6 %fusion.1 = f32[3,3,32,16]{2,3,1,0:T(8,128)S(1)} fusion(f32[3,3,16,32]{3,2,1,0:T(8,128)S(1)} %fusion.7, f32[3,3,48,32]{3,2,1,0:T(8,128)S(1)} %bitcast.56, s32[32]{0:T(128)S(1)} %compare_select_fusion.3), kind=kOutput, calls=%fused_computation.3 | convolution fusion | flops 2674176 | bytes 92288 | tf_op jit(solution)/shard_map/ky,czyj->czkj/dot_general | solution.py:24
  10.7 0.5 %fusion = f32[3,3,32,16]{2,3,1,0:T(8,128)S(1)} fusion(f32[3,3,16,32]{3,2,1,0:T(8,128)S(1)} %fusion.5, f32[3,3,48,32]{3,2,1,0:T(8,128)S(1)} %bitcast.57, s32[32]{0:T(128)S(1)} %compare_select_fusion.3), kind=kOutput, calls=%fused_computation.1 | convolution fusion | flops 2674176 | bytes 92288 | tf_op jit(solution)/shard_map/ky,czyj->czkj/dot_general | solution.py:27
  11.3 0.1 copy.23
  11.4 0.8 %reshape.212 = f32[16,1,576]{2,1,0:T(1,128)} reshape(f32[32,3,3,32]{3,2,1,0:T(4,128)S(1)} %bitcast.61) | data formatting | bytes 73728
  12.2 8.3 %all-to-all-start.1 = ((f32[16,1,576]{2,1,0:T(1,128)}), f32[16,1,576]{2,1,0:T(1,128)S(1)}, u32[]{:S(2)}, u32[]{:S(2)}) async-start(f32[16,1,576]{2,1,0:T(1,128)} %reshape.212), calls=%async_computation.1 | async-start | bytes 81920 | tf_op jit(solution)/shard_map/all_to_all | solution.py:62
  20.7 0.1 broadcast_add_fusion
  20.7 0.1 add_multiply_fusion
  20.8 0.1 broadcast_and_fusion
  20.9 0.1 and_convert_fusion
  21.0 7.0 %all-to-all-done.1 = f32[16,1,576]{2,1,0:T(1,128)S(1)} async-done(((f32[16,1,576]{2,1,0:T(1,128)}), f32[16,1,576]{2,1,0:T(1,128)S(1)}, u32[]{:S(2)}, u32[]{:S(2)}) %all-to-all-start.1) | async-done | bytes 36896 | tf_op jit(solution)/shard_map/all_to_all | solution.py:62
  28.0 0.7 %reduce.1 = f32[16,576]{1,0:T(8,128)S(1)} reduce(f32[16,1,576]{2,1,0:T(1,128)S(1)} %all-to-all-done.1, f32[]{:T(128)} %broadcast.464), dimensions={1}, to_apply=%all_to_all.30.reduce_sub_computation | reduce | bytes 73732 | tf_op jit(solution)/shard_map/all_to_all | solution.py:62
  28.6 0.1 reshape.213
  28.8 0.1 copy.25
  28.9 0.2 fusion.118
  29.1 0.1 copy.37
  29.2 0.3 %fusion.25 = f32[3,2,16,32]{3,2,1,0:T(8,128)S(1)} fusion(f32[3,48,2,16]{1,3,2,0:T(8,128)S(1)} %copy.37, s32[32]{0:T(128)S(1)} %compare_select_fusion.3), kind=kOutput, calls=%fused_computation.40 | convolution fusion | flops 1784832 | bytes 30848 | tf_op jit(solution)/shard_map/kz,czyj->ckyj/dot_general | solution.py:27
  29.5 0.1 copy.36
  29.6 0.3 %fusion.27 = f32[3,2,16,32]{3,2,1,0:T(8,128)S(1)} fusion(f32[3,48,2,16]{1,3,2,0:T(8,128)S(1)} %copy.36, s32[32]{0:T(128)S(1)} %compare_select_fusion.3), kind=kOutput, calls=%fused_computation.42 | convolution fusion | flops 1784832 | bytes 30848 | tf_op jit(solution)/shard_map/kz,czyj->ckyj/dot_general | solution.py:24
  30.0 0.3 %fusion.2 = f32[3,32,2,16]{1,3,2,0:T(8,128)S(1)} fusion(f32[3,2,16,32]{3,2,1,0:T(8,128)S(1)} %fusion.25, f32[3,48,2,16]{1,3,2,0:T(8,128)S(1)} %copy.36, s32[32]{0:T(128)S(1)} %compare_select_fusion.3), kind=kOutput, calls=%fused_computation.5 | convolution fusion | flops 1787904 | bytes 43136 | tf_op jit(solution)/shard_map/kz,czyj->ckyj/dot_general | solution.py:27
  30.3 0.3 %fusion.3 = f32[3,32,2,16]{1,3,2,0:T(8,128)S(1)} fusion(f32[3,2,16,32]{3,2,1,0:T(8,128)S(1)} %fusion.27, f32[3,48,2,16]{1,3,2,0:T(8,128)S(1)} %copy.37, s32[32]{0:T(128)S(1)} %compare_select_fusion.3), kind=kOutput, calls=%fused_computation.7 | convolution fusion | flops 1787904 | bytes 43136 | tf_op jit(solution)/shard_map/kz,czyj->ckyj/dot_general | solution.py:24
  30.6 0.1 multiply_subtract_fusion.8
  30.7 0.1 multiply_subtract_fusion.4
  30.8 0.0 copy-start
  30.8 0.9 %copy-done = f32[3,32,2,2,16]{1,4,3,2,0:T(8,128)S(1)} copy-done((f32[3,32,2,2,16]{1,4,3,2,0:T(8,128)S(1)}, f32[3,32,2,2,16]{1,4,3,2,0:T(8,128)}, u32[]{:S(2)}) %copy-start) | copy-done | bytes 24600
  31.7 0.6 %copy.29 = f32[3,32,2,2,16]{1,4,3,2,0:T(8,128)} copy(f32[3,32,2,2,16]{1,4,2,0,3:T(8,128)S(1)} %fusion.16) | data formatting | bytes 49152 | tf_op jit(solution)/shard_map/sub | solution.py:93
  (16 shorter events, 0.1 us)
Async XLA Ops:
  2.6 4.7 %all-to-all-start = ((f32[2,1,6912]{2,1,0:T(1,128)}), f32[2,1,6912]{2,1,0:T(1,128)S(1)}, u32[]{:S(2)}, u32[]{:S(2)}) async-start(f32[2,1,6912]{2,1,0:T(1,128)} %reshape.210), calls=%async_computation | async-start | bytes 110592 | tf_op jit(solution)/shard_map/all_to_all | solution.py:50
  12.2 15.8 %all-to-all-start.1 = ((f32[16,1,576]{2,1,0:T(1,128)}), f32[16,1,576]{2,1,0:T(1,128)S(1)}, u32[]{:S(2)}, u32[]{:S(2)}) async-start(f32[16,1,576]{2,1,0:T(1,128)} %reshape.212), calls=%async_computation.1 | async-start | bytes 81920 | tf_op jit(solution)/shard_map/all_to_all | solution.py:62
  30.8 0.9 %copy-start = (f32[3,32,2,2,16]{1,4,3,2,0:T(8,128)S(1)}, f32[3,32,2,2,16]{1,4,3,2,0:T(8,128)}, u32[]{:S(2)}) copy-start(f32[3,32,2,2,16]{1,4,3,2,0:T(8,128)} %param.5) | copy-start | bytes 73732
where the time goes:
time: 32.7 us; the launch traced here: 32.4 us
  starting transfers between devices  11.6 us (35%)
  waiting for transfers between devices  8.39 us (26%)
  local copies, waits for them, and re-layouts  5.12 us (16%)
  matrix products  4 us (12%)
  other arithmetic  3 us (9%)
    all_to_all x1, starting transfers between devices, per_device(): lax.all_to_all(second_pass, ('section', 'pen'), split_axis=2, concat_axis...  8.34 us
    all_to_all x1, waiting for transfers between devices, per_device(): lax.all_to_all(second_pass, ('section', 'pen'), split_axis=2, concat_axis...  7.01 us
    all_to_all x1, starting transfers between devices, per_device(): lax.all_to_all(first_pass, 'slab', split_axis=3, concat_axis=2, tiled=True)  3.28 us
    unnamed x8, local copies, waits for them, and re-layouts  3.2 us
    all_to_all x1, waiting for transfers between devices, per_device(): lax.all_to_all(first_pass, 'slab', split_axis=3, concat_axis=2, tiled=True)  1.38 us
    dot_general x2, matrix products, complex_apply(): jnp.einsum(form, cosine, imag_part, precision=highest)  0.96 us
    dot_general x2, matrix products, complex_apply(): jnp.einsum(form, sine, imag_part, precision=highest)  0.95 us
    dot_general x2, matrix products, complex_apply(): jnp.einsum(form, cosine, real_part, precision=highest)  0.89 us
  transfers between devices with their start and end apart: 2, of which 2 were waited for; matrix products, arithmetic and copies ran while one was open for 1% of the time, Pallas kernels for 0%

commit v1 on v0

--- a/solution.py
+++ b/solution.py
@@ -59,7 +59,15 @@
     halves = lax.axis_size("section")
     pens = lax.axis_size("pen")
     rows_ky = keep_count // (halves * pens)
-    block = lax.all_to_all(second_pass, ("section", "pen"), split_axis=2, concat_axis=1, tiled=True)
+    block = jnp.concatenate(
+        lax.all_to_all(
+            jnp.stack(jnp.split(second_pass, lax.axis_size(("section", "pen")), axis=2)),
+            ("section", "pen"),
+            0,
+            0,
+        ),
+        axis=1,
+    )
     out_real, out_imag = complex_apply(
         "kz,czyj->ckyj",
         cosine_table,

time: 32.7 us -> 34.3 us (1.049)
  other arithmetic: 3 us -> 4.51 us
    unnamed x0 -> x15, other arithmetic: none -> 1.42 us
    another operation x0 -> x1, local copies, waits for them, and re-layouts: none -> 0.94 us  [per_device(): jnp.stack(jnp.split(second_pass, lax.axis_size(('section', 'pen')), axis=2))]
    unnamed x8, local copies, waits for them, and re-layouts: 3.2 us -> 2.35 us
where the time goes in v1:
time: 34.3 us; the launch traced here: 33.9 us
  starting transfers between devices  11.6 us (34%)
  waiting for transfers between devices  8.39 us (24%)
  local copies, waits for them, and re-layouts  5.05 us (15%)
  other arithmetic  4.51 us (13%)
  matrix products  4.01 us (12%)
    all_to_all x1, starting transfers between devices, per_device(): lax.all_to_all(jnp.stack(jnp.split(second_pass, lax.axis_size(('section',...  8.34 us
    all_to_all x1, waiting for transfers between devices, per_device(): lax.all_to_all(jnp.stack(jnp.split(second_pass, lax.axis_size(('section',...  7.01 us
    all_to_all x1, starting transfers between devices, per_device(): lax.all_to_all(first_pass, 'slab', split_axis=3, concat_axis=2, tiled=True)  3.28 us
    unnamed x8, local copies, waits for them, and re-layouts  2.35 us
    unnamed x15, other arithmetic  1.42 us
    all_to_all x1, waiting for transfers between devices, per_device(): lax.all_to_all(first_pass, 'slab', split_axis=3, concat_axis=2, tiled=True)  1.38 us
    dot_general x2, matrix products, complex_apply(): jnp.einsum(form, cosine, imag_part, precision=highest)  0.96 us
    dot_general x2, matrix products, complex_apply(): jnp.einsum(form, sine, imag_part, precision=highest)  0.94 us
  transfers between devices with their start and end apart: 2, of which 2 were waited for; matrix products, arithmetic and copies ran while one was open for 1% of the time, Pallas kernels for 0%

profile of v1, /device:TPU:0, one launch (start us, length us, event | category | flops | bytes accessed | tf_op | source)
XLA Modules:
  0.0 33.9 jit_solution(9870490536624011459)
XLA Ops:
  0.0 0.2 cosine_multiply_fusion.1
  0.2 0.9 %multiply_subtract_fusion.2 = (f32[1,3,24,48]{3,2,1,0:T(8,128)S(1)}, f32[1,3,24,48]{3,2,1,0:T(8,128)S(1)}, f32[1,3,24,48]{3,2,1,0:T(8,128)S(1)}) fusion(f32[3,3,24,48]{3,2,1,0:T(8,128)} %param.4, f32[3,3,24,48]{3,2,1,0:T(8,128)} %param.3), kind=kLoop, calls=%fused_computation.105 | loop fusion | flops 31104 | bytes 124416 | tf_op jit(solution)/shard_map/sub | solution.py:38
  1.1 0.3 fusion.57
  1.4 0.2 copy.44
  1.6 0.9 %reshape.218 = f32[2,1,6912]{2,1,0:T(1,128)} reshape(f32[64,3,3,24]{3,2,1,0:T(4,128)S(1)} %bitcast.119) | data formatting | bytes 110592
  2.6 3.3 %all-to-all-start = ((f32[2,1,6912]{2,1,0:T(1,128)}), f32[2,1,6912]{2,1,0:T(1,128)S(1)}, u32[]{:S(2)}, u32[]{:S(2)}) async-start(f32[2,1,6912]{2,1,0:T(1,128)} %reshape.218), calls=%async_computation | async-start | bytes 110592 | tf_op jit(solution)/shard_map/all_to_all | solution.py:50
  5.9 1.4 %all-to-all-done = f32[2,1,6912]{2,1,0:T(1,128)S(1)} async-done(((f32[2,1,6912]{2,1,0:T(1,128)}), f32[2,1,6912]{2,1,0:T(1,128)S(1)}, u32[]{:S(2)}, u32[]{:S(2)}) %all-to-all-start) | async-done | bytes 55328 | tf_op jit(solution)/shard_map/all_to_all | solution.py:50
  7.2 0.5 %broadcast.464 = f32[]{:T(128)} broadcast(f32[]{:T(128)} %constant.319), dimensions={} | broadcast | bytes 8 | tf_op jit(solution)/shard_map/all_to_all | solution.py:50
  7.7 0.7 %reduce = f32[2,6912]{1,0:T(2,128)S(1)} reduce(f32[2,1,6912]{2,1,0:T(1,128)S(1)} %all-to-all-done, f32[]{:T(128)} %broadcast.464), dimensions={1}, to_apply=%all_to_all.16.reduce_sub_computation | reduce | bytes 110596 | tf_op jit(solution)/shard_map/all_to_all | solution.py:50
  8.5 0.3 reshape.219
  8.8 0.2 copy.45
  8.9 0.6 %fusion.5 = f32[3,3,16,32]{3,2,1,0:T(8,128)S(1)} fusion(f32[3,3,48,32]{3,2,1,0:T(8,128)S(1)} %bitcast.114, s32[32]{0:T(128)S(1)} %compare_select_fusion.3), kind=kOutput, calls=%fused_computation.39 | convolution fusion | flops 2669568 | bytes 73856 | tf_op jit(solution)/shard_map/ky,czyj->czkj/dot_general | solution.py:27
  9.5 0.5 %fusion.7 = f32[3,3,16,32]{3,2,1,0:T(8,128)S(1)} fusion(f32[3,3,48,32]{3,2,1,0:T(8,128)S(1)} %bitcast.115, s32[32]{0:T(128)S(1)} %compare_select_fusion.3), kind=kOutput, calls=%fused_computation.41 | convolution fusion | flops 2669568 | bytes 73856 | tf_op jit(solution)/shard_map/ky,czyj->czkj/dot_general | solution.py:24
  10.1 0.5 %fusion = f32[3,3,32,16]{2,3,1,0:T(8,128)S(1)} fusion(f32[3,3,16,32]{3,2,1,0:T(8,128)S(1)} %fusion.5, f32[3,3,48,32]{3,2,1,0:T(8,128)S(1)} %bitcast.116, s32[32]{0:T(128)S(1)} %compare_select_fusion.3), kind=kOutput, calls=%fused_computation.1 | convolution fusion | flops 2674176 | bytes 92288 | tf_op jit(solution)/shard_map/ky,czyj->czkj/dot_general | solution.py:27
  10.6 0.6 %fusion.1 = f32[3,3,32,16]{2,3,1,0:T(8,128)S(1)} fusion(f32[3,3,16,32]{3,2,1,0:T(8,128)S(1)} %fusion.7, f32[3,3,48,32]{3,2,1,0:T(8,128)S(1)} %bitcast.117, s32[32]{0:T(128)S(1)} %compare_select_fusion.3), kind=kOutput, calls=%fused_computation.3 | convolution fusion | flops 2674176 | bytes 92288 | tf_op jit(solution)/shard_map/ky,czyj->czkj/dot_general | solution.py:24
  11.3 0.1 fusion.18
  11.4 0.1 fusion.21
  11.5 0.1 fusion.24
  11.6 0.1 fusion.27
  11.7 0.1 fusion.30
  11.8 0.1 fusion.33
  11.9 0.1 fusion.36
  12.0 0.1 fusion.39
  12.1 0.1 fusion.42
  12.2 0.1 fusion.45
  12.3 0.1 fusion.48
  12.4 0.1 fusion.51
  12.6 0.1 fusion.54
  12.7 0.1 fusion.12
  12.8 0.1 fusion.56
  12.9 0.0 copy-start
  12.9 0.9 %copy.48 = f32[16,3,3,2,32]{4,3,2,1,0:T(2,128)S(1)} copy(f32[16,3,3,2,32]{3,4,2,1,0:T(8,128)S(1)} %fusion.56) | data formatting | bytes 73728 | tf_op jit(solution)/shard_map/stack | solution.py:64
  13.8 0.8 %reshape.220 = f32[16,1,576]{2,1,0:T(1,128)} reshape(f32[16,3,3,2,32]{4,3,2,1,0:T(2,128)S(1)} %copy.48) | data formatting | bytes 73728
  14.6 8.3 %all-to-all-start.1 = ((f32[16,1,576]{2,1,0:T(1,128)}), f32[16,1,576]{2,1,0:T(1,128)S(1)}, u32[]{:S(2)}, u32[]{:S(2)}) async-start(f32[16,1,576]{2,1,0:T(1,128)} %reshape.220), calls=%async_computation.1 | async-start | bytes 81920 | tf_op jit(solution)/shard_map/all_to_all | solution.py:63
  23.1 0.1 broadcast_add_fusion
  23.2 0.1 add_multiply_fusion
  23.3 0.1 broadcast_and_fusion
  23.3 0.1 and_convert_fusion
  23.4 7.0 %all-to-all-done.1 = f32[16,1,576]{2,1,0:T(1,128)S(1)} async-done(((f32[16,1,576]{2,1,0:T(1,128)}), f32[16,1,576]{2,1,0:T(1,128)S(1)}, u32[]{:S(2)}, u32[]{:S(2)}) %all-to-all-start.1) | async-done | bytes 36896 | tf_op jit(solution)/shard_map/all_to_all | solution.py:63
  30.4 0.7 %reduce.1 = f32[16,576]{1,0:T(8,128)S(1)} reduce(f32[16,1,576]{2,1,0:T(1,128)S(1)} %all-to-all-done.1, f32[]{:T(128)} %broadcast.464), dimensions={1}, to_apply=%all_to_all.20.reduce_sub_computation | reduce | bytes 73732 | tf_op jit(solution)/shard_map/all_to_all | solution.py:63
  31.1 0.1 reshape.221
  31.3 0.2 fusion.165
  31.5 0.1 copy.61
  31.6 0.3 %fusion.72 = f32[3,2,16,32]{3,2,1,0:T(8,128)S(1)} fusion(f32[3,48,2,16]{1,3,2,0:T(8,128)S(1)} %copy.61, s32[32]{0:T(128)S(1)} %compare_select_fusion.3), kind=kOutput, calls=%fused_computation.117 | convolution fusion | flops 1784832 | bytes 30848 | tf_op jit(solution)/shard_map/kz,czyj->ckyj/dot_general | solution.py:27
  31.9 0.1 copy.60
  32.0 0.3 %fusion.74 = f32[3,2,16,32]{3,2,1,0:T(8,128)S(1)} fusion(f32[3,48,2,16]{1,3,2,0:T(8,128)S(1)} %copy.60, s32[32]{0:T(128)S(1)} %compare_select_fusion.3), kind=kOutput, calls=%fused_computation.119 | convolution fusion | flops 1784832 | bytes 30848 | tf_op jit(solution)/shard_map/kz,czyj->ckyj/dot_general | solution.py:24
  32.4 0.3 fusion.2
  32.7 0.3 fusion.3
  33.0 0.1 multiply_subtract_fusion.8
  33.1 0.1 multiply_subtract_fusion.4
  33.2 0.0 copy-done
  33.3 0.6 %copy.53 = f32[3,32,2,2,16]{1,4,3,2,0:T(8,128)} copy(f32[3,32,2,2,16]{1,4,2,0,3:T(8,128)S(1)} %fusion.63) | data formatting | bytes 49152 | tf_op jit(solution)/shard_map/sub | solution.py:101
  (16 shorter events, 0.2 us)
Async XLA Ops:
  2.6 4.7 %all-to-all-start = ((f32[2,1,6912]{2,1,0:T(1,128)}), f32[2,1,6912]{2,1,0:T(1,128)S(1)}, u32[]{:S(2)}, u32[]{:S(2)}) async-start(f32[2,1,6912]{2,1,0:T(1,128)} %reshape.218), calls=%async_computation | async-start | bytes 110592 | tf_op jit(solution)/shard_map/all_to_all | solution.py:50
  12.9 20.3 %copy-start = (f32[3,32,2,2,16]{1,4,3,2,0:T(8,128)S(1)}, f32[3,32,2,2,16]{1,4,3,2,0:T(8,128)}, u32[]{:S(2)}) copy-start(f32[3,32,2,2,16]{1,4,3,2,0:T(8,128)} %param.5) | copy-start | bytes 73732
  14.6 15.8 %all-to-all-start.1 = ((f32[16,1,576]{2,1,0:T(1,128)}), f32[16,1,576]{2,1,0:T(1,128)S(1)}, u32[]{:S(2)}, u32[]{:S(2)}) async-start(f32[16,1,576]{2,1,0:T(1,128)} %reshape.220), calls=%async_computation.1 | async-start | bytes 81920 | tf_op jit(solution)/shard_map/all_to_all | solution.py:63
